TPU v7x, 32 devices: a whole 2x2x4 slice. The times are simulated.
32 devices in a mesh: grp: 2 (over core), tile: 16 (over z, y, x).
Axes of the slice: x: 2, y: 2, z: 4, core: 2. Of those that a mesh axis runs over, the one named last changes fastest.
Arguments:
- attn_input: bfloat16 [2048, 4096], P(('grp', 'tile')), may hold values from -9 to 9
- mlp_input: bfloat16 [2048, 4096], P(('grp', 'tile')), may hold values from -9 to 9
Outputs:
- hess_attn: float32 [16, 1024, 1024], P('tile', 'grp')
- hess_mlp: float32 [16, 1024, 1024], P('tile', 'grp')
All inputs are finite; a program needn't handle non-finite values.
Results may differ from a plain program's by a relative error of at most 0.0003.
Values may be sent and summed in bfloat16 or wider, within the bound.
A program may use at most 192 MiB of HBM per device.

v0:
```python
import jax
import jax.numpy as jnp
from jax import lax
from jax.sharding import PartitionSpec as P

ROWB = 4
TOKB = 32


def tile_first(inputs, tile_count):
    tok_rows, feat_width = inputs.shape
    col_blocks = tile_count // ROWB
    row_width = feat_width // ROWB
    col_width = feat_width // col_blocks

    def accumulate(turn_idx, partial_value):
        tok_block = lax.dynamic_slice_in_dim(inputs, turn_idx * TOKB, TOKB, 0)
        row_parts = tok_block.reshape(TOKB, ROWB, row_width).transpose(1, 0, 2)
        row_send = jnp.repeat(row_parts, col_blocks, axis=0)
        col_parts = tok_block.reshape(TOKB, col_blocks, col_width).transpose(1, 0, 2)
        col_send = jnp.tile(col_parts, (ROWB, 1, 1))
        rows_in, cols_in = (
            lax.all_to_all(row_send, "tile", split_axis=0, concat_axis=0, tiled=True),
            lax.all_to_all(col_send, "tile", split_axis=0, concat_axis=0, tiled=True),
        )
        rows_flat = rows_in.reshape(tile_count * TOKB, row_width)
        cols_flat = cols_in.reshape(tile_count * TOKB, col_width)
        return partial_value + lax.dot_general(
            rows_flat, cols_flat, (((0,), (0,)), ((), ())), preferred_element_type=jnp.float32
        )

    partial_value = lax.fori_loop(
        0, tok_rows // TOKB, accumulate, jnp.zeros((row_width, col_width), jnp.float32)
    )
    shares = lax.psum_scatter(partial_value, "grp", scatter_dimension=0, tiled=True)
    return shares[None]


def hessian_share(inputs):
    tile_count = lax.axis_size("tile")
    group_count = lax.axis_size("grp")
    norm_factor = 2.0 / (inputs.shape[0] * tile_count * group_count)
    shares = tile_first(inputs, tile_count)
    return shares * norm_factor


def body(attn_input, mlp_input):
    return (hessian_share(attn_input), hessian_share(mlp_input))


def solution(mesh):
    in_specs = (P(("grp", "tile"), None), P(("grp", "tile"), None))
    out_specs = (P("tile", "grp", None), P("tile", "grp", None))
    return jax.shard_map(body, mesh=mesh, in_specs=in_specs, out_specs=out_specs, check_vma=False)
```

profile of v0, /device:TPU:0, one launch (start us, length us, event | category | flops | bytes accessed | tf_op | source)
XLA Modules:
  0.0 291.0 jit_solution(9503920627443665375)
XLA Ops:
  7.2 0.0 reduce-scatter.5.cloned.1.call-start
  7.2 133.3 %while.29 = (s32[]{:T(128)}, f32[1024,1024]{1,0:T(8,128)}, bf16[64,4096]{1,0:T(8,128)(2,1)}, s32[]{:T(128)}, s32[]{:T(128)}, /*index=5*/s32[]{:T(128)}, s32[]{:T(128)}) while((s32[]{:T(128)}, f32[1024,1024]{1,0:T(8,128)}, bf16[64,4096]{1,0:T(8,128)(2,1)}, s32[]{:T(128)}, s32[]{:T(128)}, /*index=5*/s32[]{:T(128)}, s32[]{:T(128)}) %tuple.66), condition=%wide.region_4.0_spmd.clone, body=%wide.region_3.0_spmd.clone.sunk | while | flops 1075838976 | bytes 19923112 | solution.py:32
  7.2 1.0 constant_dynamic-slice_fusion.5
  8.2 0.2 reshape.65
  8.4 0.1 copy.11
  8.5 0.1 tile.49
  8.6 34.5 %all_to_all.45 = bf16[16,32,1024]{2,1,0:T(8,128)(2,1)S(1)} all-to-all(bf16[16,32,1024]{2,1,0:T(8,128)(2,1)S(1)} %bitcast.42), channel_id=1, replica_groups=mesh['grp'=2,'tile'=16] {'tile'}, dimensions={0} | all-to-all | bytes 2097152 | tf_op jit(solution)/shard_map/while/body/eval_jaxpr/all_to_all | solution.py:24
  43.1 1.1 broadcast_in_dim.21
  44.2 3.9 %all-to-all-start.2 = ((bf16[16,32,1024]{2,1,0:T(8,128)(2,1)}), bf16[16,32,1024]{2,1,0:T(8,128)(2,1)S(1)}, u32[]{:S(2)}, u32[]{:S(2)}) async-start(bf16[16,32,1024]{2,1,0:T(8,128)(2,1)} %bitcast.40), calls=%async_computation.2 | async-start | bytes 2097152 | tf_op jit(solution)/shard_map/while/body/eval_jaxpr/all_to_all | solution.py:23
  48.1 23.7 %all-to-all-done.2 = bf16[16,32,1024]{2,1,0:T(8,128)(2,1)S(1)} async-done(((bf16[16,32,1024]{2,1,0:T(8,128)(2,1)}), bf16[16,32,1024]{2,1,0:T(8,128)(2,1)S(1)}, u32[]{:S(2)}, u32[]{:S(2)}) %all-to-all-start.2) | async-done | bytes 1048608 | tf_op jit(solution)/shard_map/while/body/eval_jaxpr/all_to_all | solution.py:23
  71.8 3.3 %bitcast_add_fusion.5 = f32[1024,1024]{1,0:T(8,128)} fusion(f32[1024,1024]{1,0:T(8,128)} %get-tuple-element.235, bf16[16,32,1024]{2,1,0:T(8,128)(2,1)S(1)} %all-to-all-done.2, bf16[16,32,1024]{2,1,0:T(8,128)(2,1)S(1)} %all_to_all.45, pred[]{:T(512)S(6)} %compare.7), kind=kOutput, calls=%fused_computation.2.clone.1 | convolution fusion | flops 1075838976 | bytes 10485761 | tf_op jit(solution)/shard_map/while/body/eval_jaxpr/dot_general | solution.py:28
  75.1 1.0 constant_dynamic-slice_fusion.5
  76.1 0.2 reshape.65
  76.2 0.1 copy.11
  76.3 0.1 tile.49
  76.5 30.7 %all_to_all.45 = bf16[16,32,1024]{2,1,0:T(8,128)(2,1)S(1)} all-to-all(bf16[16,32,1024]{2,1,0:T(8,128)(2,1)S(1)} %bitcast.42), channel_id=1, replica_groups=mesh['grp'=2,'tile'=16] {'tile'}, dimensions={0} | all-to-all | bytes 2097152 | tf_op jit(solution)/shard_map/while/body/eval_jaxpr/all_to_all | solution.py:24
  107.1 1.1 broadcast_in_dim.21
  108.2 3.9 %all-to-all-start.2 = ((bf16[16,32,1024]{2,1,0:T(8,128)(2,1)}), bf16[16,32,1024]{2,1,0:T(8,128)(2,1)S(1)}, u32[]{:S(2)}, u32[]{:S(2)}) async-start(bf16[16,32,1024]{2,1,0:T(8,128)(2,1)} %bitcast.40), calls=%async_computation.2 | async-start | bytes 2097152 | tf_op jit(solution)/shard_map/while/body/eval_jaxpr/all_to_all | solution.py:23
  112.1 23.0 %all-to-all-done.2 = bf16[16,32,1024]{2,1,0:T(8,128)(2,1)S(1)} async-done(((bf16[16,32,1024]{2,1,0:T(8,128)(2,1)}), bf16[16,32,1024]{2,1,0:T(8,128)(2,1)S(1)}, u32[]{:S(2)}, u32[]{:S(2)}) %all-to-all-start.2) | async-done | bytes 1048608 | tf_op jit(solution)/shard_map/while/body/eval_jaxpr/all_to_all | solution.py:23
  135.1 5.5 %bitcast_add_fusion.5 = f32[1024,1024]{1,0:T(8,128)} fusion(f32[1024,1024]{1,0:T(8,128)} %get-tuple-element.235, bf16[16,32,1024]{2,1,0:T(8,128)(2,1)S(1)} %all-to-all-done.2, bf16[16,32,1024]{2,1,0:T(8,128)(2,1)S(1)} %all_to_all.45, pred[]{:T(512)S(6)} %compare.7), kind=kOutput, calls=%fused_computation.2.clone.1 | convolution fusion | flops 1075838976 | bytes 10485761 | tf_op jit(solution)/shard_map/while/body/eval_jaxpr/dot_general | solution.py:28
  140.6 0.0 copy-start
  140.6 0.0 reduce-scatter.5.cloned.1.call-update
  140.6 0.0 reduce-scatter.3.cloned.1.call-start
  140.7 1.0 copy-done
  141.6 126.8 %while.28 = (s32[]{:T(128)}, f32[1024,1024]{1,0:T(8,128)}, bf16[64,4096]{1,0:T(8,128)(2,1)S(1)}, s32[]{:T(128)}, s32[]{:T(128)}, /*index=5*/s32[]{:T(128)}, s32[]{:T(128)}) while((s32[]{:T(128)}, f32[1024,1024]{1,0:T(8,128)}, bf16[64,4096]{1,0:T(8,128)(2,1)S(1)}, s32[]{:T(128)}, s32[]{:T(128)}, /*index=5*/s32[]{:T(128)}, ...), condition=%wide.region_1.0_spmd.clone, body=%wide.region_0.0_spmd.clone.sunk | while | flops 1075838976 | bytes 19923112 | solution.py:32
  141.6 0.2 reshape.64
  141.8 0.1 copy.10
  141.9 0.1 tile.48
  142.0 30.7 %all_to_all.44 = bf16[16,32,1024]{2,1,0:T(8,128)(2,1)S(1)} all-to-all(bf16[16,32,1024]{2,1,0:T(8,128)(2,1)S(1)} %bitcast.43), channel_id=1, replica_groups=mesh['grp'=2,'tile'=16] {'tile'}, dimensions={0} | all-to-all | bytes 2097152 | tf_op jit(solution)/shard_map/while/body/eval_jaxpr/all_to_all | solution.py:24
  172.8 1.1 broadcast_in_dim.20
  173.9 3.9 %all-to-all-start = ((bf16[16,32,1024]{2,1,0:T(8,128)(2,1)}), bf16[16,32,1024]{2,1,0:T(8,128)(2,1)S(1)}, u32[]{:S(2)}, u32[]{:S(2)}) async-start(bf16[16,32,1024]{2,1,0:T(8,128)(2,1)} %bitcast.34), calls=%async_computation | async-start | bytes 2097152 | tf_op jit(solution)/shard_map/while/body/eval_jaxpr/all_to_all | solution.py:23
  177.8 22.9 %all-to-all-done = bf16[16,32,1024]{2,1,0:T(8,128)(2,1)S(1)} async-done(((bf16[16,32,1024]{2,1,0:T(8,128)(2,1)}), bf16[16,32,1024]{2,1,0:T(8,128)(2,1)S(1)}, u32[]{:S(2)}, u32[]{:S(2)}) %all-to-all-start) | async-done | bytes 1048608 | tf_op jit(solution)/shard_map/while/body/eval_jaxpr/all_to_all | solution.py:23
  200.7 3.2 %bitcast_add_fusion.4 = f32[1024,1024]{1,0:T(8,128)} fusion(f32[1024,1024]{1,0:T(8,128)} %get-tuple-element.214, bf16[16,32,1024]{2,1,0:T(8,128)(2,1)S(1)} %all-to-all-done, bf16[16,32,1024]{2,1,0:T(8,128)(2,1)S(1)} %all_to_all.44, pred[]{:T(512)S(6)} %compare.6), kind=kOutput, calls=%fused_computation.clone.1 | convolution fusion | flops 1075838976 | bytes 10485761 | tf_op jit(solution)/shard_map/while/body/eval_jaxpr/dot_general | solution.py:28
  203.9 0.2 reshape.64
  204.1 0.1 copy.10
  204.2 0.1 tile.48
  204.3 30.7 %all_to_all.44 = bf16[16,32,1024]{2,1,0:T(8,128)(2,1)S(1)} all-to-all(bf16[16,32,1024]{2,1,0:T(8,128)(2,1)S(1)} %bitcast.43), channel_id=1, replica_groups=mesh['grp'=2,'tile'=16] {'tile'}, dimensions={0} | all-to-all | bytes 2097152 | tf_op jit(solution)/shard_map/while/body/eval_jaxpr/all_to_all | solution.py:24
  235.0 1.1 broadcast_in_dim.20
  236.1 3.9 %all-to-all-start = ((bf16[16,32,1024]{2,1,0:T(8,128)(2,1)}), bf16[16,32,1024]{2,1,0:T(8,128)(2,1)S(1)}, u32[]{:S(2)}, u32[]{:S(2)}) async-start(bf16[16,32,1024]{2,1,0:T(8,128)(2,1)} %bitcast.34), calls=%async_computation | async-start | bytes 2097152 | tf_op jit(solution)/shard_map/while/body/eval_jaxpr/all_to_all | solution.py:23
  240.0 22.9 %all-to-all-done = bf16[16,32,1024]{2,1,0:T(8,128)(2,1)S(1)} async-done(((bf16[16,32,1024]{2,1,0:T(8,128)(2,1)}), bf16[16,32,1024]{2,1,0:T(8,128)(2,1)S(1)}, u32[]{:S(2)}, u32[]{:S(2)}) %all-to-all-start) | async-done | bytes 1048608 | tf_op jit(solution)/shard_map/while/body/eval_jaxpr/all_to_all | solution.py:23
  262.9 5.4 %bitcast_add_fusion.4 = f32[1024,1024]{1,0:T(8,128)} fusion(f32[1024,1024]{1,0:T(8,128)} %get-tuple-element.214, bf16[16,32,1024]{2,1,0:T(8,128)(2,1)S(1)} %all-to-all-done, bf16[16,32,1024]{2,1,0:T(8,128)(2,1)S(1)} %all_to_all.44, pred[]{:T(512)S(6)} %compare.6), kind=kOutput, calls=%fused_computation.clone.1 | convolution fusion | flops 1075838976 | bytes 10485761 | tf_op jit(solution)/shard_map/while/body/eval_jaxpr/dot_general | solution.py:28
  268.4 0.0 reduce-scatter.3.cloned.1.call-update
  268.4 0.0 reduce-scatter.5.cloned.1.call-done
  268.4 3.2 %multiply_bitcast_fusion = f32[1,512,1024]{2,1,0:T(8,128)} fusion(f32[512,1024]{1,0:T(8,128)} %reduce-scatter.5.cloned.1.call-done), kind=kLoop, calls=%fused_computation.4 | loop fusion | flops 524288 | bytes 4194304 | tf_op jit(solution)/shard_map/mul | solution.py:44
  271.6 9.3 %reduce-scatter.3.cloned.1.call-done = f32[512,1024]{1,0:T(8,128)} async-done(((f32[1024,1024]{1,0:T(8,128)}), f32[512,1024]{1,0:T(8,128)}) %reduce-scatter.3.cloned.1.call-update) | async-done | bytes 2097168 | tf_op jit(solution)/shard_map/reduce_scatter | solution.py:35
  281.0 3.2 %multiply_bitcast_fusion.1 = f32[1,512,1024]{2,1,0:T(8,128)} fusion(f32[512,1024]{1,0:T(8,128)} %reduce-scatter.3.cloned.1.call-done), kind=kLoop, calls=%fused_computation.5 | loop fusion | flops 524288 | bytes 4194304 | tf_op jit(solution)/shard_map/mul | solution.py:44
  (4 shorter events, 0.0 us)
Async XLA Ops:
  7.2 261.3 %reduce-scatter.5.cloned.1.call-start = ((), (), s32[]{:S(2)}) async-start(), calls=%async_computation.7 | async-start | bytes 6291456 | tf_op jit(solution)/shard_map/reduce_scatter | solution.py:35
  44.2 27.6 %all-to-all-start.2 = ((bf16[16,32,1024]{2,1,0:T(8,128)(2,1)}), bf16[16,32,1024]{2,1,0:T(8,128)(2,1)S(1)}, u32[]{:S(2)}, u32[]{:S(2)}) async-start(bf16[16,32,1024]{2,1,0:T(8,128)(2,1)} %bitcast.40), calls=%async_computation.2 | async-start | bytes 2097152 | tf_op jit(solution)/shard_map/while/body/eval_jaxpr/all_to_all | solution.py:23
  108.2 26.9 %all-to-all-start.2 = ((bf16[16,32,1024]{2,1,0:T(8,128)(2,1)}), bf16[16,32,1024]{2,1,0:T(8,128)(2,1)S(1)}, u32[]{:S(2)}, u32[]{:S(2)}) async-start(bf16[16,32,1024]{2,1,0:T(8,128)(2,1)} %bitcast.40), calls=%async_computation.2 | async-start | bytes 2097152 | tf_op jit(solution)/shard_map/while/body/eval_jaxpr/all_to_all | solution.py:23
  140.6 1.0 copy-start
  140.6 140.4 %reduce-scatter.3.cloned.1.call-start = ((), (), s32[]{:S(2)}) async-start(), calls=%async_computation.6 | async-start | bytes 6291456 | tf_op jit(solution)/shard_map/reduce_scatter | solution.py:35
  173.9 26.8 %all-to-all-start = ((bf16[16,32,1024]{2,1,0:T(8,128)(2,1)}), bf16[16,32,1024]{2,1,0:T(8,128)(2,1)S(1)}, u32[]{:S(2)}, u32[]{:S(2)}) async-start(bf16[16,32,1024]{2,1,0:T(8,128)(2,1)} %bitcast.34), calls=%async_computation | async-start | bytes 2097152 | tf_op jit(solution)/shard_map/while/body/eval_jaxpr/all_to_all | solution.py:23
  236.1 26.8 %all-to-all-start = ((bf16[16,32,1024]{2,1,0:T(8,128)(2,1)}), bf16[16,32,1024]{2,1,0:T(8,128)(2,1)S(1)}, u32[]{:S(2)}, u32[]{:S(2)}) async-start(bf16[16,32,1024]{2,1,0:T(8,128)(2,1)} %bitcast.34), calls=%async_computation | async-start | bytes 2097152 | tf_op jit(solution)/shard_map/while/body/eval_jaxpr/all_to_all | solution.py:23
Sparse Core Ops, SparseCore 0:
  140.7 12.4 reduce-scatter.4
  268.5 12.4 reduce-scatter.2
where the time goes:
time: 292 us; the launch traced here: 291 us
  blocking collectives  127 us (43%)
  waiting for transfers between devices  102 us (35%)
  matrix products  17.4 us (6%)
  starting transfers between devices  15.7 us (5%)
  between operations  14.1 us (5%)
  local copies, waits for them, and re-layouts  8.85 us (3%)
  other arithmetic  6.44 us (2%)
    all_to_all x4, blocking collectives, accumulate(): lax.all_to_all(col_send, 'tile', split_axis=0, concat_axis=0, tiled=True)  127 us
    all_to_all x4, waiting for transfers between devices, accumulate(): lax.all_to_all(row_send, 'tile', split_axis=0, concat_axis=0, tiled=True)  92.4 us
    dot_general x4, matrix products, accumulate(): lax.dot_general(rows_flat, cols_flat, (((0,), (0,)), ((), ())), preferred...  17.4 us
    all_to_all x4, starting transfers between devices, accumulate(): lax.all_to_all(row_send, 'tile', split_axis=0, concat_axis=0, tiled=True)  15.6 us
    reduce_scatter x2, waiting for transfers between devices, tile_first(): lax.psum_scatter(partial_value, 'grp', scatter_dimension=0, tiled=True)  9.37 us
    mul x2, other arithmetic, hessian_share(): return shares * norm_factor  6.44 us
  transfers between devices with their start and end apart: 6, of which 5 were waited for; matrix products, arithmetic and copies ran while one was open for 5% of the time, Pallas kernels for 0%

commit v1 on v0

--- a/solution.py
+++ b/solution.py
@@ -5,6 +5,22 @@
 
 ROWB = 4
 TOKB = 32
+
+
+def pairwise_exchange(value, axis, split, join):
+    ways, here = (lax.axis_size(axis), lax.axis_index(axis))
+    width = value.shape[split] // ways
+    lengths = list(value.shape)
+    lengths[split] = width
+    height = lengths[join]
+    lengths[join] = height * ways
+    full = jnp.zeros(lengths, value.dtype)
+    for mask in range(ways):
+        part = lax.dynamic_slice_in_dim(value, (here ^ mask) * width, width, axis=split)
+        if mask:
+            part = lax.ppermute(part, axis, [(d, d ^ mask) for d in range(ways)])
+        full = lax.dynamic_update_slice_in_dim(full, part, (here ^ mask) * height, axis=join)
+    return full
 
 
 def tile_first(inputs, tile_count):
@@ -21,7 +37,7 @@
         col_send = jnp.tile(col_parts, (ROWB, 1, 1))
         rows_in, cols_in = (
             lax.all_to_all(row_send, "tile", split_axis=0, concat_axis=0, tiled=True),
-            lax.all_to_all(col_send, "tile", split_axis=0, concat_axis=0, tiled=True),
+            pairwise_exchange(col_send, "tile", 0, 0),
         )
         rows_flat = rows_in.reshape(tile_count * TOKB, row_width)
         cols_flat = cols_in.reshape(tile_count * TOKB, col_width)

time: 292 us -> 266 us (0.911)
  starting transfers between devices: 15.7 us -> 149 us
  blocking collectives: 127 us -> 0 us
  waiting for transfers between devices: 102 us -> 56.4 us
  local copies, waits for them, and re-layouts: 8.85 us -> 20.1 us
    ppermute x0 -> x60, starting transfers between devices: none -> 128 us  [pairwise_exchange(): part = lax.ppermute(part, axis, [(d, d ^ mask) for d in range(ways)])]
    all_to_all x4 -> x0, blocking collectives: 127 us -> none  [accumulate(): lax.all_to_all(col_send, 'tile', split_axis=0, concat_axis=0, tiled=True)]
    all_to_all x4, waiting for transfers between devices: 92.4 us -> 0.01 us  [accumulate(): lax.all_to_all(row_send, 'tile', split_axis=0, concat_axis=0, tiled=True)]
    ppermute x0 -> x60, waiting for transfers between devices: none -> 48.9 us  [pairwise_exchange(): part = lax.ppermute(part, axis, [(d, d ^ mask) for d in range(ways)])]
    dynamic_update_slice x0 -> x60, local copies, waits for them, and re-layouts: none -> 8.88 us  [pairwise_exchange(): lax.dynamic_update_slice_in_dim(full, part, (here ^ mask) * height, axis=...]
    all_to_all x4, starting transfers between devices: 15.6 us -> 20.1 us  [accumulate(): lax.all_to_all(row_send, 'tile', split_axis=0, concat_axis=0, tiled=True)]
  transfers between devices with their start and end apart: 6 -> 66, of which waited for: 5 -> 22; matrix products, arithmetic and copies ran while one was open for 5% -> 10% of each run, Pallas kernels for 0% -> 0%
where the time goes in v1:
time: 266 us; the launch traced here: 264 us
  starting transfers between devices  149 us (56%)
  waiting for transfers between devices  56.4 us (21%)
  local copies, waits for them, and re-layouts  20.1 us (8%)
  matrix products  17.6 us (7%)
  between operations  14.1 us (5%)
  other arithmetic  6.44 us (2%)
    ppermute x60, starting transfers between devices, pairwise_exchange(): part = lax.ppermute(part, axis, [(d, d ^ mask) for d in range(ways)])  128 us
    ppermute x60, waiting for transfers between devices, pairwise_exchange(): part = lax.ppermute(part, axis, [(d, d ^ mask) for d in range(ways)])  48.9 us
    all_to_all x4, starting transfers between devices, accumulate(): lax.all_to_all(row_send, 'tile', split_axis=0, concat_axis=0, tiled=True)  20.1 us
    dot_general x4, matrix products, accumulate(): lax.dot_general(rows_flat, cols_flat, (((0,), (0,)), ((), ())), preferred...  17.6 us
    dynamic_update_slice x60, local copies, waits for them, and re-layouts, pairwise_exchange(): lax.dynamic_update_slice_in_dim(full, part, (here ^ mask) * height, axis=...  8.88 us
    reduce_scatter x2, waiting for transfers between devices, tile_first(): lax.psum_scatter(partial_value, 'grp', scatter_dimension=0, tiled=True)  7.46 us
    mul x2, other arithmetic, hessian_share(): return shares * norm_factor  6.44 us
  transfers between devices with their start and end apart: 66, of which 22 were waited for; matrix products, arithmetic and copies ran while one was open for 10% of the time, Pallas kernels for 0%

profile of v1, /device:TPU:0, one launch (start us, length us, event | category | flops | bytes accessed | tf_op | source)
XLA Modules:
  0.0 264.4 jit_solution(4995387418618076525)
XLA Ops:
  7.2 122.6 %while.29 = (s32[]{:T(128)}, f32[1024,1024]{1,0:T(8,128)}, bf16[64,4096]{1,0:T(8,128)(2,1)}, s32[]{:T(128)}, s32[]{:T(128)}, /*index=5*/s32[]{:T(128)}, s32[]{:T...) while((s32[]{:T(128)}, f32[1024,1024]{1,0:T(8,128)}, ...), condition=%wide.region_4.0_spmd.clone, body=%wide.region_3.0_spmd.clone.sunk | while | flops 1075839104 | bytes 26871544 | solution.py:48
  9.6 8.3 %all-to-all-start.1 = ((bf16[16,32,1024]{2,1,0:T(8,128)(2,1)}), bf16[16,32,1024]{2,1,0:T(8,128)(2,1)S(1)}, u32[]{:S(2)}, u32[]{:S(2)}) async-start(bf16[16,32,1024]{2,1,0:T(8,128)(2,1)} %bitcast.40), calls=%async_computation.1 | async-start | bytes 2097152 | tf_op jit(solution)/shard_map/while/body/eval_jaxpr/all_to_all | solution.py:39
  18.4 1.9 collective-permute-start.15
  22.0 1.8 collective-permute-start.18
  25.3 2.4 collective-permute-start.20
  27.7 1.9 collective-permute-done.16
  30.6 4.2 %collective-permute-start.22 = (bf16[1,32,1024]{2,1,0:T(8,128)(2,1)S(1)}, bf16[1,32,1024]{2,1,0:T(8,128)(2,1)S(1)}, u32[]{:S(2)}, u32[]{:S(2)}) collective-permute-start(bf16[1,32,1024]{2,1,0:T(8,128)(2,1)S(1)} %get-tuple-element.294), channel_id=1, source_target_pairs={{0,8},{1,9},{2,10},{3,11},{4,12},{5,13},{6,14},{7,15},{8,0},{9,1},... | collective-permute-start | bytes 196616 | tf_op jit(solution)/shard_map/while/body/eval_jaxpr/ppermute | solution.py:21
  34.8 2.6 collective-permute-done.18
  37.5 5.7 %collective-permute-start.23 = (bf16[1,32,1024]{2,1,0:T(8,128)(2,1)S(1)}, bf16[1,32,1024]{2,1,0:T(8,128)(2,1)S(1)}, u32[]{:S(2)}, u32[]{:S(2)}) collective-permute-start(bf16[1,32,1024]{2,1,0:T(8,128)(2,1)S(1)} %get-tuple-element.295), channel_id=1, source_target_pairs={{0,9},{1,8},{2,11},{3,10},{4,13},{5,12},{6,15},{7,14},{8,1},{9,0},... | collective-permute-start | bytes 196616 | tf_op jit(solution)/shard_map/while/body/eval_jaxpr/ppermute | solution.py:21
  43.2 2.5 collective-permute-start.24
  45.6 1.6 collective-permute-start.25
  48.0 5.9 %collective-permute-done.22 = bf16[1,32,1024]{2,1,0:T(8,128)(2,1)S(1)} collective-permute-done((bf16[1,32,1024]{2,1,0:T(8,128)(2,1)S(1)}, bf16[1,32,1024]{2,1,0:T(8,128)(2,1)S(1)}, u32[]{:S(2)}, u32[]{:S(2)}) %collective-permute-start.22) | collective-permute-done | bytes 65568 | tf_op jit(solution)/shard_map/while/body/eval_jaxpr/ppermute | solution.py:21
  53.9 2.6 collective-permute-start.27
  56.5 3.3 %collective-permute-start.28 = (bf16[1,32,1024]{2,1,0:T(8,128)(2,1)S(1)}, bf16[1,32,1024]{2,1,0:T(8,128)(2,1)S(1)}, u32[]{:S(2)}, u32[]{:S(2)}) collective-permute-start(bf16[1,32,1024]{2,1,0:T(8,128)(2,1)S(1)} %get-tuple-element.300), channel_id=1, source_target_pairs={{0,14},{1,15},{2,12},{3,13},{4,10},{5,11},{6,8},{7,9},{8,6},{9,7},... | collective-permute-start | bytes 196616 | tf_op jit(solution)/shard_map/while/body/eval_jaxpr/ppermute | solution.py:21
  59.8 1.6 collective-permute-start.29
  61.4 2.0 collective-permute-done.28
  63.5 4.3 %collective-permute-done.29 = bf16[1,32,1024]{2,1,0:T(8,128)(2,1)S(1)} collective-permute-done((bf16[1,32,1024]{2,1,0:T(8,128)(2,1)S(1)}, bf16[1,32,1024]{2,1,0:T(8,128)(2,1)S(1)}, u32[]{:S(2)}, u32[]{:S(2)}) %collective-permute-start.29) | collective-permute-done | bytes 65568 | tf_op jit(solution)/shard_map/while/body/eval_jaxpr/ppermute | solution.py:21
  67.8 3.3 %bitcast_add_fusion.5 = f32[1024,1024]{1,0:T(8,128)} fusion(f32[1024,1024]{1,0:T(8,128)} %get-tuple-element.399, bf16[16,32,1024]{2,1,0:T(8,128)(2,1)S(1)} %all-to-all-done.1, bf16[16,32,1024]{2,1,0:T(8,128)(2,1)S(1)} %constant_dynamic-update-slice_fusion.89, pred[]{:T(512)S(6)} %compare.7), kind=kOutput, calls=%fused_computation.33.clone.1 | convolution fusion | flops 1075838976 | bytes 10485761 | tf_op jit(solution)/shard_map/while/body/eval_jaxpr/dot_general | solution.py:44
  73.5 3.7 %all-to-all-start.1 = ((bf16[16,32,1024]{2,1,0:T(8,128)(2,1)}), bf16[16,32,1024]{2,1,0:T(8,128)(2,1)S(1)}, u32[]{:S(2)}, u32[]{:S(2)}) async-start(bf16[16,32,1024]{2,1,0:T(8,128)(2,1)} %bitcast.40), calls=%async_computation.1 | async-start | bytes 2097152 | tf_op jit(solution)/shard_map/while/body/eval_jaxpr/all_to_all | solution.py:39
  77.7 1.8 collective-permute-start.15
  81.2 1.7 collective-permute-start.18
  84.4 2.4 collective-permute-start.20
  88.2 3.5 %collective-permute-start.22 = (bf16[1,32,1024]{2,1,0:T(8,128)(2,1)S(1)}, bf16[1,32,1024]{2,1,0:T(8,128)(2,1)S(1)}, u32[]{:S(2)}, u32[]{:S(2)}) collective-permute-start(bf16[1,32,1024]{2,1,0:T(8,128)(2,1)S(1)} %get-tuple-element.294), channel_id=1, source_target_pairs={{0,8},{1,9},{2,10},{3,11},{4,12},{5,13},{6,14},{7,15},{8,0},{9,1},... | collective-permute-start | bytes 196616 | tf_op jit(solution)/shard_map/while/body/eval_jaxpr/ppermute | solution.py:21
  91.7 4.4 %collective-permute-done.18 = bf16[1,32,1024]{2,1,0:T(8,128)(2,1)S(1)} collective-permute-done((bf16[1,32,1024]{2,1,0:T(8,128)(2,1)S(1)}, bf16[1,32,1024]{2,1,0:T(8,128)(2,1)S(1)}, u32[]{:S(2)}, u32[]{:S(2)}) %collective-permute-start.18) | collective-permute-done | bytes 65568 | tf_op jit(solution)/shard_map/while/body/eval_jaxpr/ppermute | solution.py:21
  96.1 6.2 %collective-permute-start.23 = (bf16[1,32,1024]{2,1,0:T(8,128)(2,1)S(1)}, bf16[1,32,1024]{2,1,0:T(8,128)(2,1)S(1)}, u32[]{:S(2)}, u32[]{:S(2)}) collective-permute-start(bf16[1,32,1024]{2,1,0:T(8,128)(2,1)S(1)} %get-tuple-element.295), channel_id=1, source_target_pairs={{0,9},{1,8},{2,11},{3,10},{4,13},{5,12},{6,15},{7,14},{8,1},{9,0},... | collective-permute-start | bytes 196616 | tf_op jit(solution)/shard_map/while/body/eval_jaxpr/ppermute | solution.py:21
  102.4 2.4 collective-permute-start.24
  107.2 2.5 collective-permute-done.22
  112.8 3.4 %collective-permute-start.28 = (bf16[1,32,1024]{2,1,0:T(8,128)(2,1)S(1)}, bf16[1,32,1024]{2,1,0:T(8,128)(2,1)S(1)}, u32[]{:S(2)}, u32[]{:S(2)}) collective-permute-start(bf16[1,32,1024]{2,1,0:T(8,128)(2,1)S(1)} %get-tuple-element.300), channel_id=1, source_target_pairs={{0,14},{1,15},{2,12},{3,13},{4,10},{5,11},{6,8},{7,9},{8,6},{9,7},... | collective-permute-start | bytes 196616 | tf_op jit(solution)/shard_map/while/body/eval_jaxpr/ppermute | solution.py:21
  116.3 2.0 collective-permute-start.29
  120.0 4.3 %collective-permute-done.29 = bf16[1,32,1024]{2,1,0:T(8,128)(2,1)S(1)} collective-permute-done((bf16[1,32,1024]{2,1,0:T(8,128)(2,1)S(1)}, bf16[1,32,1024]{2,1,0:T(8,128)(2,1)S(1)}, u32[]{:S(2)}, u32[]{:S(2)}) %collective-permute-start.29) | collective-permute-done | bytes 65568 | tf_op jit(solution)/shard_map/while/body/eval_jaxpr/ppermute | solution.py:21
  124.3 5.5 %bitcast_add_fusion.5 = f32[1024,1024]{1,0:T(8,128)} fusion(f32[1024,1024]{1,0:T(8,128)} %get-tuple-element.399, bf16[16,32,1024]{2,1,0:T(8,128)(2,1)S(1)} %all-to-all-done.1, bf16[16,32,1024]{2,1,0:T(8,128)(2,1)S(1)} %constant_dynamic-update-slice_fusion.89, pred[]{:T(512)S(6)} %compare.7), kind=kOutput, calls=%fused_computation.33.clone.1 | convolution fusion | flops 1075838976 | bytes 10485761 | tf_op jit(solution)/shard_map/while/body/eval_jaxpr/dot_general | solution.py:44
  130.9 112.8 %while.28 = (s32[]{:T(128)}, f32[1024,1024]{1,0:T(8,128)}, bf16[64,4096]{1,0:T(8,128)(2,1)S(1)}, s32[]{:T(128)}, s32[]{:T(128)}, /*index=5*/s32[]{:T(128)}, s32[...) while((s32[]{:T(128)}, f32[1024,1024]{1,0:T(8,128)}, ...), condition=%wide.region_1.0_spmd.clone, body=%wide.region_0.0_spmd.clone.sunk | while | flops 1075839104 | bytes 26871544 | solution.py:48
  132.3 4.0 %all-to-all-start = ((bf16[16,32,1024]{2,1,0:T(8,128)(2,1)}), bf16[16,32,1024]{2,1,0:T(8,128)(2,1)S(1)}, u32[]{:S(2)}, u32[]{:S(2)}) async-start(bf16[16,32,1024]{2,1,0:T(8,128)(2,1)} %bitcast.34), calls=%async_computation | async-start | bytes 2097152 | tf_op jit(solution)/shard_map/while/body/eval_jaxpr/all_to_all | solution.py:39
  137.4 1.8 collective-permute-start
  140.9 1.8 collective-permute-start.3
  144.2 2.4 collective-permute-start.5
  148.5 2.9 %collective-permute-start.7 = (bf16[1,32,1024]{2,1,0:T(8,128)(2,1)S(1)}, bf16[1,32,1024]{2,1,0:T(8,128)(2,1)S(1)}, u32[]{:S(2)}, u32[]{:S(2)}) collective-permute-start(bf16[1,32,1024]{2,1,0:T(8,128)(2,1)S(1)} %get-tuple-element.275), channel_id=1, source_target_pairs={{0,8},{1,9},{2,10},{3,11},{4,12},{5,13},{6,14},{7,15},{8,0},{9,1},... | collective-permute-start | bytes 196616 | tf_op jit(solution)/shard_map/while/body/eval_jaxpr/ppermute | solution.py:21
  152.3 3.2 %collective-permute-done.3 = bf16[1,32,1024]{2,1,0:T(8,128)(2,1)} collective-permute-done((bf16[1,32,1024]{2,1,0:T(8,128)(2,1)S(1)}, bf16[1,32,1024]{2,1,0:T(8,128)(2,1)}, u32[]{:S(2)}, u32[]{:S(2)}) %collective-permute-start.3) | collective-permute-done | bytes 65568 | tf_op jit(solution)/shard_map/while/body/eval_jaxpr/ppermute | solution.py:21
  155.5 6.1 %collective-permute-start.8 = (bf16[1,32,1024]{2,1,0:T(8,128)(2,1)S(1)}, bf16[1,32,1024]{2,1,0:T(8,128)(2,1)S(1)}, u32[]{:S(2)}, u32[]{:S(2)}) collective-permute-start(bf16[1,32,1024]{2,1,0:T(8,128)(2,1)S(1)} %get-tuple-element.276), channel_id=1, source_target_pairs={{0,9},{1,8},{2,11},{3,10},{4,13},{5,12},{6,15},{7,14},{8,1},{9,0},... | collective-permute-start | bytes 196616 | tf_op jit(solution)/shard_map/while/body/eval_jaxpr/ppermute | solution.py:21
  162.5 1.6 collective-permute-start.9
  164.9 2.4 collective-permute-start.10
  167.4 4.8 %collective-permute-start.12 = (bf16[1,32,1024]{2,1,0:T(8,128)(2,1)S(1)}, bf16[1,32,1024]{2,1,0:T(8,128)(2,1)S(1)}, u32[]{:S(2)}, u32[]{:S(2)}) collective-permute-start(bf16[1,32,1024]{2,1,0:T(8,128)(2,1)S(1)} %get-tuple-element.280), channel_id=1, source_target_pairs={{0,13},{1,12},{2,15},{3,14},{4,9},{5,8},{6,11},{7,10},{8,5},{9,4},... | collective-permute-start | bytes 196616 | tf_op jit(solution)/shard_map/while/body/eval_jaxpr/ppermute | solution.py:21
  172.2 2.5 collective-permute-start.13
  174.8 2.3 collective-permute-start.14
  179.3 3.4 %collective-permute-done.14 = bf16[1,32,1024]{2,1,0:T(8,128)(2,1)S(1)} collective-permute-done((bf16[1,32,1024]{2,1,0:T(8,128)(2,1)S(1)}, bf16[1,32,1024]{2,1,0:T(8,128)(2,1)S(1)}, u32[]{:S(2)}, u32[]{:S(2)}) %collective-permute-start.14) | collective-permute-done | bytes 65568 | tf_op jit(solution)/shard_map/while/body/eval_jaxpr/ppermute | solution.py:21
  182.8 3.3 %bitcast_add_fusion.4 = f32[1024,1024]{1,0:T(8,128)} fusion(f32[1024,1024]{1,0:T(8,128)} %get-tuple-element.327, bf16[16,32,1024]{2,1,0:T(8,128)(2,1)S(1)} %all-to-all-done, bf16[16,32,1024]{2,1,0:T(8,128)(2,1)S(1)} %constant_dynamic-update-slice_fusion.74, pred[]{:T(512)S(6)} %compare.6), kind=kOutput, calls=%fused_computation.clone.1 | convolution fusion | flops 1075838976 | bytes 10485761 | tf_op jit(solution)/shard_map/while/body/eval_jaxpr/dot_general | solution.py:44
  187.5 4.1 %all-to-all-start = ((bf16[16,32,1024]{2,1,0:T(8,128)(2,1)}), bf16[16,32,1024]{2,1,0:T(8,128)(2,1)S(1)}, u32[]{:S(2)}, u32[]{:S(2)}) async-start(bf16[16,32,1024]{2,1,0:T(8,128)(2,1)} %bitcast.34), calls=%async_computation | async-start | bytes 2097152 | tf_op jit(solution)/shard_map/while/body/eval_jaxpr/all_to_all | solution.py:39
  192.8 2.2 collective-permute-start
  196.4 1.7 collective-permute-start.3
  198.1 1.8 collective-permute-start.4
  199.9 2.0 collective-permute-start.5
  204.3 2.6 collective-permute-start.7
  207.7 3.0 %collective-permute-done.3 = bf16[1,32,1024]{2,1,0:T(8,128)(2,1)} collective-permute-done((bf16[1,32,1024]{2,1,0:T(8,128)(2,1)S(1)}, bf16[1,32,1024]{2,1,0:T(8,128)(2,1)}, u32[]{:S(2)}, u32[]{:S(2)}) %collective-permute-start.3) | collective-permute-done | bytes 65568 | tf_op jit(solution)/shard_map/while/body/eval_jaxpr/ppermute | solution.py:21
  210.7 6.2 %collective-permute-start.8 = (bf16[1,32,1024]{2,1,0:T(8,128)(2,1)S(1)}, bf16[1,32,1024]{2,1,0:T(8,128)(2,1)S(1)}, u32[]{:S(2)}, u32[]{:S(2)}) collective-permute-start(bf16[1,32,1024]{2,1,0:T(8,128)(2,1)S(1)} %get-tuple-element.276), channel_id=1, source_target_pairs={{0,9},{1,8},{2,11},{3,10},{4,13},{5,12},{6,15},{7,14},{8,1},{9,0},... | collective-permute-start | bytes 196616 | tf_op jit(solution)/shard_map/while/body/eval_jaxpr/ppermute | solution.py:21
  217.8 1.6 collective-permute-start.9
  220.2 2.4 collective-permute-start.10
  222.7 4.8 %collective-permute-start.12 = (bf16[1,32,1024]{2,1,0:T(8,128)(2,1)S(1)}, bf16[1,32,1024]{2,1,0:T(8,128)(2,1)S(1)}, u32[]{:S(2)}, u32[]{:S(2)}) collective-permute-start(bf16[1,32,1024]{2,1,0:T(8,128)(2,1)S(1)} %get-tuple-element.280), channel_id=1, source_target_pairs={{0,13},{1,12},{2,15},{3,14},{4,9},{5,8},{6,11},{7,10},{8,5},{9,4},... | collective-permute-start | bytes 196616 | tf_op jit(solution)/shard_map/while/body/eval_jaxpr/ppermute | solution.py:21
  227.5 2.5 collective-permute-start.13
  230.2 2.2 collective-permute-start.14
  234.6 3.5 %collective-permute-done.14 = bf16[1,32,1024]{2,1,0:T(8,128)(2,1)S(1)} collective-permute-done((bf16[1,32,1024]{2,1,0:T(8,128)(2,1)S(1)}, bf16[1,32,1024]{2,1,0:T(8,128)(2,1)S(1)}, u32[]{:S(2)}, u32[]{:S(2)}) %collective-permute-start.14) | collective-permute-done | bytes 65568 | tf_op jit(solution)/shard_map/while/body/eval_jaxpr/ppermute | solution.py:21
  238.1 5.5 %bitcast_add_fusion.4 = f32[1024,1024]{1,0:T(8,128)} fusion(f32[1024,1024]{1,0:T(8,128)} %get-tuple-element.327, bf16[16,32,1024]{2,1,0:T(8,128)(2,1)S(1)} %all-to-all-done, bf16[16,32,1024]{2,1,0:T(8,128)(2,1)S(1)} %constant_dynamic-update-slice_fusion.74, pred[]{:T(512)S(6)} %compare.6), kind=kOutput, calls=%fused_computation.clone.1 | convolution fusion | flops 1075838976 | bytes 10485761 | tf_op jit(solution)/shard_map/while/body/eval_jaxpr/dot_general | solution.py:44
  243.7 3.2 %multiply_bitcast_fusion = f32[1,512,1024]{2,1,0:T(8,128)} fusion(f32[512,1024]{1,0:T(8,128)} %reduce-scatter.5.cloned.1.call-done), kind=kLoop, calls=%fused_computation.66 | loop fusion | flops 524288 | bytes 4194304 | tf_op jit(solution)/shard_map/mul | solution.py:60
  246.9 7.4 %reduce-scatter.3.cloned.1.call-done = f32[512,1024]{1,0:T(8,128)} async-done(((f32[1024,1024]{1,0:T(8,128)}), f32[512,1024]{1,0:T(8,128)}) %reduce-scatter.3.cloned.1.call-update) | async-done | bytes 2097168 | tf_op jit(solution)/shard_map/reduce_scatter | solution.py:51
  254.3 3.2 %multiply_bitcast_fusion.1 = f32[1,512,1024]{2,1,0:T(8,128)} fusion(f32[512,1024]{1,0:T(8,128)} %reduce-scatter.3.cloned.1.call-done), kind=kLoop, calls=%fused_computation.67 | loop fusion | flops 524288 | bytes 4194304 | tf_op jit(solution)/shard_map/mul | solution.py:60
  (170 shorter events, 47.1 us)
Async XLA Ops:
  7.2 236.5 %reduce-scatter.5.cloned.1.call-start = ((), (), s32[]{:S(2)}) async-start(), calls=%async_computation.5 | async-start | bytes 6291456 | tf_op jit(solution)/shard_map/reduce_scatter | solution.py:51
  9.6 58.2 %all-to-all-start.1 = ((bf16[16,32,1024]{2,1,0:T(8,128)(2,1)}), bf16[16,32,1024]{2,1,0:T(8,128)(2,1)S(1)}, u32[]{:S(2)}, u32[]{:S(2)}) async-start(bf16[16,32,1024]{2,1,0:T(8,128)(2,1)} %bitcast.40), calls=%async_computation.1 | async-start | bytes 2097152 | tf_op jit(solution)/shard_map/while/body/eval_jaxpr/all_to_all | solution.py:39
  18.4 6.9 %collective-permute-start.15 = (bf16[1,32,1024]{2,1,0:T(8,128)(2,1)S(1)}, bf16[1,32,1024]{2,1,0:T(8,128)(2,1)S(1)}, u32[]{:S(2)}, u32[]{:S(2)}) collective-permute-start(bf16[1,32,1024]{2,1,0:T(8,128)(2,1)S(1)} %get-tuple-element.287), channel_id=1, source_target_pairs={{0,1},{1,0},{2,3},{3,2},{4,5},{5,4},{6,7},{7,6},{8,9},{9,8},{10,11... | collective-permute-start | bytes 196616 | tf_op jit(solution)/shard_map/while/body/eval_jaxpr/ppermute | solution.py:21
  20.3 9.2 %collective-permute-start.16 = (bf16[1,32,1024]{2,1,0:T(8,128)(2,1)S(1)}, bf16[1,32,1024]{2,1,0:T(8,128)(2,1)S(1)}, u32[]{:S(2)}, u32[]{:S(2)}) collective-permute-start(bf16[1,32,1024]{2,1,0:T(8,128)(2,1)S(1)} %get-tuple-element.288), channel_id=1, source_target_pairs={{0,2},{1,3},{2,0},{3,1},{4,6},{5,7},{6,4},{7,5},{8,10},{9,11},{10,... | collective-permute-start | bytes 196616 | tf_op jit(solution)/shard_map/while/body/eval_jaxpr/ppermute | solution.py:21
  21.8 8.8 %collective-permute-start.17 = (bf16[1,32,1024]{2,1,0:T(8,128)(2,1)S(1)}, bf16[1,32,1024]{2,1,0:T(8,128)(2,1)S(1)}, u32[]{:S(2)}, u32[]{:S(2)}) collective-permute-start(bf16[1,32,1024]{2,1,0:T(8,128)(2,1)S(1)} %get-tuple-element.289), channel_id=1, source_target_pairs={{0,3},{1,2},{2,1},{3,0},{4,7},{5,6},{6,5},{7,4},{8,11},{9,10},{10,... | collective-permute-start | bytes 196616 | tf_op jit(solution)/shard_map/while/body/eval_jaxpr/ppermute | solution.py:21
  22.0 15.5 %collective-permute-start.18 = (bf16[1,32,1024]{2,1,0:T(8,128)(2,1)S(1)}, bf16[1,32,1024]{2,1,0:T(8,128)(2,1)S(1)}, u32[]{:S(2)}, u32[]{:S(2)}) collective-permute-start(bf16[1,32,1024]{2,1,0:T(8,128)(2,1)S(1)} %get-tuple-element.290), channel_id=1, source_target_pairs={{0,4},{1,5},{2,6},{3,7},{4,0},{5,1},{6,2},{7,3},{8,12},{9,13},{10,... | collective-permute-start | bytes 196616 | tf_op jit(solution)/shard_map/while/body/eval_jaxpr/ppermute | solution.py:21
  23.8 19.3 %collective-permute-start.19 = (bf16[1,32,1024]{2,1,0:T(8,128)(2,1)S(1)}, bf16[1,32,1024]{2,1,0:T(8,128)(2,1)S(1)}, u32[]{:S(2)}, u32[]{:S(2)}) collective-permute-start(bf16[1,32,1024]{2,1,0:T(8,128)(2,1)S(1)} %get-tuple-element.291), channel_id=1, source_target_pairs={{0,5},{1,4},{2,7},{3,6},{4,1},{5,0},{6,3},{7,2},{8,13},{9,12},{10,... | collective-permute-start | bytes 196616 | tf_op jit(solution)/shard_map/while/body/eval_jaxpr/ppermute | solution.py:21
  25.3 20.3 %collective-permute-start.20 = (bf16[1,32,1024]{2,1,0:T(8,128)(2,1)S(1)}, bf16[1,32,1024]{2,1,0:T(8,128)(2,1)S(1)}, u32[]{:S(2)}, u32[]{:S(2)}) collective-permute-start(bf16[1,32,1024]{2,1,0:T(8,128)(2,1)S(1)} %get-tuple-element.292), channel_id=1, source_target_pairs={{0,6},{1,7},{2,4},{3,5},{4,2},{5,3},{6,0},{7,1},{8,14},{9,15},{10,... | collective-permute-start | bytes 196616 | tf_op jit(solution)/shard_map/while/body/eval_jaxpr/ppermute | solution.py:21
  29.6 17.6 %collective-permute-start.21 = (bf16[1,32,1024]{2,1,0:T(8,128)(2,1)S(1)}, bf16[1,32,1024]{2,1,0:T(8,128)(2,1)S(1)}, u32[]{:S(2)}, u32[]{:S(2)}) collective-permute-start(bf16[1,32,1024]{2,1,0:T(8,128)(2,1)S(1)} %get-tuple-element.293), channel_id=1, source_target_pairs={{0,7},{1,6},{2,5},{3,4},{4,3},{5,2},{6,1},{7,0},{8,15},{9,14},{10,... | collective-permute-start | bytes 196616 | tf_op jit(solution)/shard_map/while/body/eval_jaxpr/ppermute | solution.py:21
  30.6 23.3 %collective-permute-start.22 = (bf16[1,32,1024]{2,1,0:T(8,128)(2,1)S(1)}, bf16[1,32,1024]{2,1,0:T(8,128)(2,1)S(1)}, u32[]{:S(2)}, u32[]{:S(2)}) collective-permute-start(bf16[1,32,1024]{2,1,0:T(8,128)(2,1)S(1)} %get-tuple-element.294), channel_id=1, source_target_pairs={{0,8},{1,9},{2,10},{3,11},{4,12},{5,13},{6,14},{7,15},{8,0},{9,1},... | collective-permute-start | bytes 196616 | tf_op jit(solution)/shard_map/while/body/eval_jaxpr/ppermute | solution.py:21
  37.5 19.0 %collective-permute-start.23 = (bf16[1,32,1024]{2,1,0:T(8,128)(2,1)S(1)}, bf16[1,32,1024]{2,1,0:T(8,128)(2,1)S(1)}, u32[]{:S(2)}, u32[]{:S(2)}) collective-permute-start(bf16[1,32,1024]{2,1,0:T(8,128)(2,1)S(1)} %get-tuple-element.295), channel_id=1, source_target_pairs={{0,9},{1,8},{2,11},{3,10},{4,13},{5,12},{6,15},{7,14},{8,1},{9,0},... | collective-permute-start | bytes 196616 | tf_op jit(solution)/shard_map/while/body/eval_jaxpr/ppermute | solution.py:21
  43.2 16.6 %collective-permute-start.24 = (bf16[1,32,1024]{2,1,0:T(8,128)(2,1)S(1)}, bf16[1,32,1024]{2,1,0:T(8,128)(2,1)S(1)}, u32[]{:S(2)}, u32[]{:S(2)}) collective-permute-start(bf16[1,32,1024]{2,1,0:T(8,128)(2,1)S(1)} %get-tuple-element.296), channel_id=1, source_target_pairs={{0,10},{1,11},{2,8},{3,9},{4,14},{5,15},{6,12},{7,13},{8,2},{9,3},... | collective-permute-start | bytes 196616 | tf_op jit(solution)/shard_map/while/body/eval_jaxpr/ppermute | solution.py:21
  45.6 15.7 %collective-permute-start.25 = (bf16[1,32,1024]{2,1,0:T(8,128)(2,1)S(1)}, bf16[1,32,1024]{2,1,0:T(8,128)(2,1)S(1)}, u32[]{:S(2)}, u32[]{:S(2)}) collective-permute-start(bf16[1,32,1024]{2,1,0:T(8,128)(2,1)S(1)} %get-tuple-element.297), channel_id=1, source_target_pairs={{0,11},{1,10},{2,9},{3,8},{4,15},{5,14},{6,13},{7,12},{8,3},{9,2},... | collective-permute-start | bytes 196616 | tf_op jit(solution)/shard_map/while/body/eval_jaxpr/ppermute | solution.py:21
  47.2 14.2 %collective-permute-start.26 = (bf16[1,32,1024]{2,1,0:T(8,128)(2,1)S(1)}, bf16[1,32,1024]{2,1,0:T(8,128)(2,1)S(1)}, u32[]{:S(2)}, u32[]{:S(2)}) collective-permute-start(bf16[1,32,1024]{2,1,0:T(8,128)(2,1)S(1)} %get-tuple-element.298), channel_id=1, source_target_pairs={{0,12},{1,13},{2,14},{3,15},{4,8},{5,9},{6,10},{7,11},{8,4},{9,5},... | collective-permute-start | bytes 196616 | tf_op jit(solution)/shard_map/while/body/eval_jaxpr/ppermute | solution.py:21
  53.9 7.5 %collective-permute-start.27 = (bf16[1,32,1024]{2,1,0:T(8,128)(2,1)S(1)}, bf16[1,32,1024]{2,1,0:T(8,128)(2,1)S(1)}, u32[]{:S(2)}, u32[]{:S(2)}) collective-permute-start(bf16[1,32,1024]{2,1,0:T(8,128)(2,1)S(1)} %get-tuple-element.299), channel_id=1, source_target_pairs={{0,13},{1,12},{2,15},{3,14},{4,9},{5,8},{6,11},{7,10},{8,5},{9,4},... | collective-permute-start | bytes 196616 | tf_op jit(solution)/shard_map/while/body/eval_jaxpr/ppermute | solution.py:21
  56.5 7.0 %collective-permute-start.28 = (bf16[1,32,1024]{2,1,0:T(8,128)(2,1)S(1)}, bf16[1,32,1024]{2,1,0:T(8,128)(2,1)S(1)}, u32[]{:S(2)}, u32[]{:S(2)}) collective-permute-start(bf16[1,32,1024]{2,1,0:T(8,128)(2,1)S(1)} %get-tuple-element.300), channel_id=1, source_target_pairs={{0,14},{1,15},{2,12},{3,13},{4,10},{5,11},{6,8},{7,9},{8,6},{9,7},... | collective-permute-start | bytes 196616 | tf_op jit(solution)/shard_map/while/body/eval_jaxpr/ppermute | solution.py:21
  59.8 8.0 %collective-permute-start.29 = (bf16[1,32,1024]{2,1,0:T(8,128)(2,1)S(1)}, bf16[1,32,1024]{2,1,0:T(8,128)(2,1)S(1)}, u32[]{:S(2)}, u32[]{:S(2)}) collective-permute-start(bf16[1,32,1024]{2,1,0:T(8,128)(2,1)S(1)} %get-tuple-element.301), channel_id=1, source_target_pairs={{0,15},{1,14},{2,13},{3,12},{4,11},{5,10},{6,9},{7,8},{8,7},{9,6},... | collective-permute-start | bytes 196616 | tf_op jit(solution)/shard_map/while/body/eval_jaxpr/ppermute | solution.py:21
  73.5 50.8 %all-to-all-start.1 = ((bf16[16,32,1024]{2,1,0:T(8,128)(2,1)}), bf16[16,32,1024]{2,1,0:T(8,128)(2,1)S(1)}, u32[]{:S(2)}, u32[]{:S(2)}) async-start(bf16[16,32,1024]{2,1,0:T(8,128)(2,1)} %bitcast.40), calls=%async_computation.1 | async-start | bytes 2097152 | tf_op jit(solution)/shard_map/while/body/eval_jaxpr/all_to_all | solution.py:39
  79.5 7.4 %collective-permute-start.16 = (bf16[1,32,1024]{2,1,0:T(8,128)(2,1)S(1)}, bf16[1,32,1024]{2,1,0:T(8,128)(2,1)S(1)}, u32[]{:S(2)}, u32[]{:S(2)}) collective-permute-start(bf16[1,32,1024]{2,1,0:T(8,128)(2,1)S(1)} %get-tuple-element.288), channel_id=1, source_target_pairs={{0,2},{1,3},{2,0},{3,1},{4,6},{5,7},{6,4},{7,5},{8,10},{9,11},{10,... | collective-permute-start | bytes 196616 | tf_op jit(solution)/shard_map/while/body/eval_jaxpr/ppermute | solution.py:21
  80.9 7.3 %collective-permute-start.17 = (bf16[1,32,1024]{2,1,0:T(8,128)(2,1)S(1)}, bf16[1,32,1024]{2,1,0:T(8,128)(2,1)S(1)}, u32[]{:S(2)}, u32[]{:S(2)}) collective-permute-start(bf16[1,32,1024]{2,1,0:T(8,128)(2,1)S(1)} %get-tuple-element.289), channel_id=1, source_target_pairs={{0,3},{1,2},{2,1},{3,0},{4,7},{5,6},{6,5},{7,4},{8,11},{9,10},{10,... | collective-permute-start | bytes 196616 | tf_op jit(solution)/shard_map/while/body/eval_jaxpr/ppermute | solution.py:21
  81.2 14.9 %collective-permute-start.18 = (bf16[1,32,1024]{2,1,0:T(8,128)(2,1)S(1)}, bf16[1,32,1024]{2,1,0:T(8,128)(2,1)S(1)}, u32[]{:S(2)}, u32[]{:S(2)}) collective-permute-start(bf16[1,32,1024]{2,1,0:T(8,128)(2,1)S(1)} %get-tuple-element.290), channel_id=1, source_target_pairs={{0,4},{1,5},{2,6},{3,7},{4,0},{5,1},{6,2},{7,3},{8,12},{9,13},{10,... | collective-permute-start | bytes 196616 | tf_op jit(solution)/shard_map/while/body/eval_jaxpr/ppermute | solution.py:21
  83.0 19.4 %collective-permute-start.19 = (bf16[1,32,1024]{2,1,0:T(8,128)(2,1)S(1)}, bf16[1,32,1024]{2,1,0:T(8,128)(2,1)S(1)}, u32[]{:S(2)}, u32[]{:S(2)}) collective-permute-start(bf16[1,32,1024]{2,1,0:T(8,128)(2,1)S(1)} %get-tuple-element.291), channel_id=1, source_target_pairs={{0,5},{1,4},{2,7},{3,6},{4,1},{5,0},{6,3},{7,2},{8,13},{9,12},{10,... | collective-permute-start | bytes 196616 | tf_op jit(solution)/shard_map/while/body/eval_jaxpr/ppermute | solution.py:21
  84.4 20.4 %collective-permute-start.20 = (bf16[1,32,1024]{2,1,0:T(8,128)(2,1)S(1)}, bf16[1,32,1024]{2,1,0:T(8,128)(2,1)S(1)}, u32[]{:S(2)}, u32[]{:S(2)}) collective-permute-start(bf16[1,32,1024]{2,1,0:T(8,128)(2,1)S(1)} %get-tuple-element.292), channel_id=1, source_target_pairs={{0,6},{1,7},{2,4},{3,5},{4,2},{5,3},{6,0},{7,1},{8,14},{9,15},{10,... | collective-permute-start | bytes 196616 | tf_op jit(solution)/shard_map/while/body/eval_jaxpr/ppermute | solution.py:21
  86.9 19.5 %collective-permute-start.21 = (bf16[1,32,1024]{2,1,0:T(8,128)(2,1)S(1)}, bf16[1,32,1024]{2,1,0:T(8,128)(2,1)S(1)}, u32[]{:S(2)}, u32[]{:S(2)}) collective-permute-start(bf16[1,32,1024]{2,1,0:T(8,128)(2,1)S(1)} %get-tuple-element.293), channel_id=1, source_target_pairs={{0,7},{1,6},{2,5},{3,4},{4,3},{5,2},{6,1},{7,0},{8,15},{9,14},{10,... | collective-permute-start | bytes 196616 | tf_op jit(solution)/shard_map/while/body/eval_jaxpr/ppermute | solution.py:21
  88.2 21.5 %collective-permute-start.22 = (bf16[1,32,1024]{2,1,0:T(8,128)(2,1)S(1)}, bf16[1,32,1024]{2,1,0:T(8,128)(2,1)S(1)}, u32[]{:S(2)}, u32[]{:S(2)}) collective-permute-start(bf16[1,32,1024]{2,1,0:T(8,128)(2,1)S(1)} %get-tuple-element.294), channel_id=1, source_target_pairs={{0,8},{1,9},{2,10},{3,11},{4,12},{5,13},{6,14},{7,15},{8,0},{9,1},... | collective-permute-start | bytes 196616 | tf_op jit(solution)/shard_map/while/body/eval_jaxpr/ppermute | solution.py:21
  96.1 16.6 %collective-permute-start.23 = (bf16[1,32,1024]{2,1,0:T(8,128)(2,1)S(1)}, bf16[1,32,1024]{2,1,0:T(8,128)(2,1)S(1)}, u32[]{:S(2)}, u32[]{:S(2)}) collective-permute-start(bf16[1,32,1024]{2,1,0:T(8,128)(2,1)S(1)} %get-tuple-element.295), channel_id=1, source_target_pairs={{0,9},{1,8},{2,11},{3,10},{4,13},{5,12},{6,15},{7,14},{8,1},{9,0},... | collective-permute-start | bytes 196616 | tf_op jit(solution)/shard_map/while/body/eval_jaxpr/ppermute | solution.py:21
  102.4 13.9 %collective-permute-start.24 = (bf16[1,32,1024]{2,1,0:T(8,128)(2,1)S(1)}, bf16[1,32,1024]{2,1,0:T(8,128)(2,1)S(1)}, u32[]{:S(2)}, u32[]{:S(2)}) collective-permute-start(bf16[1,32,1024]{2,1,0:T(8,128)(2,1)S(1)} %get-tuple-element.296), channel_id=1, source_target_pairs={{0,10},{1,11},{2,8},{3,9},{4,14},{5,15},{6,12},{7,13},{8,2},{9,3},... | collective-permute-start | bytes 196616 | tf_op jit(solution)/shard_map/while/body/eval_jaxpr/ppermute | solution.py:21
  104.8 14.7 %collective-permute-start.25 = (bf16[1,32,1024]{2,1,0:T(8,128)(2,1)S(1)}, bf16[1,32,1024]{2,1,0:T(8,128)(2,1)S(1)}, u32[]{:S(2)}, u32[]{:S(2)}) collective-permute-start(bf16[1,32,1024]{2,1,0:T(8,128)(2,1)S(1)} %get-tuple-element.297), channel_id=1, source_target_pairs={{0,11},{1,10},{2,9},{3,8},{4,15},{5,14},{6,13},{7,12},{8,3},{9,2},... | collective-permute-start | bytes 196616 | tf_op jit(solution)/shard_map/while/body/eval_jaxpr/ppermute | solution.py:21
  106.4 13.1 %collective-permute-start.26 = (bf16[1,32,1024]{2,1,0:T(8,128)(2,1)S(1)}, bf16[1,32,1024]{2,1,0:T(8,128)(2,1)S(1)}, u32[]{:S(2)}, u32[]{:S(2)}) collective-permute-start(bf16[1,32,1024]{2,1,0:T(8,128)(2,1)S(1)} %get-tuple-element.298), channel_id=1, source_target_pairs={{0,12},{1,13},{2,14},{3,15},{4,8},{5,9},{6,10},{7,11},{8,4},{9,5},... | collective-permute-start | bytes 196616 | tf_op jit(solution)/shard_map/while/body/eval_jaxpr/ppermute | solution.py:21
  109.8 9.8 %collective-permute-start.27 = (bf16[1,32,1024]{2,1,0:T(8,128)(2,1)S(1)}, bf16[1,32,1024]{2,1,0:T(8,128)(2,1)S(1)}, u32[]{:S(2)}, u32[]{:S(2)}) collective-permute-start(bf16[1,32,1024]{2,1,0:T(8,128)(2,1)S(1)} %get-tuple-element.299), channel_id=1, source_target_pairs={{0,13},{1,12},{2,15},{3,14},{4,9},{5,8},{6,11},{7,10},{8,5},{9,4},... | collective-permute-start | bytes 196616 | tf_op jit(solution)/shard_map/while/body/eval_jaxpr/ppermute | solution.py:21
  112.8 7.2 %collective-permute-start.28 = (bf16[1,32,1024]{2,1,0:T(8,128)(2,1)S(1)}, bf16[1,32,1024]{2,1,0:T(8,128)(2,1)S(1)}, u32[]{:S(2)}, u32[]{:S(2)}) collective-permute-start(bf16[1,32,1024]{2,1,0:T(8,128)(2,1)S(1)} %get-tuple-element.300), channel_id=1, source_target_pairs={{0,14},{1,15},{2,12},{3,13},{4,10},{5,11},{6,8},{7,9},{8,6},{9,7},... | collective-permute-start | bytes 196616 | tf_op jit(solution)/shard_map/while/body/eval_jaxpr/ppermute | solution.py:21
  116.3 8.0 %collective-permute-start.29 = (bf16[1,32,1024]{2,1,0:T(8,128)(2,1)S(1)}, bf16[1,32,1024]{2,1,0:T(8,128)(2,1)S(1)}, u32[]{:S(2)}, u32[]{:S(2)}) collective-permute-start(bf16[1,32,1024]{2,1,0:T(8,128)(2,1)S(1)} %get-tuple-element.301), channel_id=1, source_target_pairs={{0,15},{1,14},{2,13},{3,12},{4,11},{5,10},{6,9},{7,8},{8,7},{9,6},... | collective-permute-start | bytes 196616 | tf_op jit(solution)/shard_map/while/body/eval_jaxpr/ppermute | solution.py:21
  129.8 124.5 %reduce-scatter.3.cloned.1.call-start = ((), (), s32[]{:S(2)}) async-start(), calls=%async_computation.4 | async-start | bytes 6291456 | tf_op jit(solution)/shard_map/reduce_scatter | solution.py:51
  132.3 50.5 %all-to-all-start = ((bf16[16,32,1024]{2,1,0:T(8,128)(2,1)}), bf16[16,32,1024]{2,1,0:T(8,128)(2,1)S(1)}, u32[]{:S(2)}, u32[]{:S(2)}) async-start(bf16[16,32,1024]{2,1,0:T(8,128)(2,1)} %bitcast.34), calls=%async_computation | async-start | bytes 2097152 | tf_op jit(solution)/shard_map/while/body/eval_jaxpr/all_to_all | solution.py:39
  139.2 8.2 %collective-permute-start.1 = (bf16[1,32,1024]{2,1,0:T(8,128)(2,1)S(1)}, bf16[1,32,1024]{2,1,0:T(8,128)(2,1)}, u32[]{:S(2)}, u32[]{:S(2)}) collective-permute-start(bf16[1,32,1024]{2,1,0:T(8,128)(2,1)S(1)} %get-tuple-element.269), channel_id=1, source_target_pairs={{0,2},{1,3},{2,0},{3,1},{4,6},{5,7},{6,4},{7,5},{8,10},{9,11},{10,... | collective-permute-start | bytes 196616 | tf_op jit(solution)/shard_map/while/body/eval_jaxpr/ppermute | solution.py:21
  140.7 7.8 %collective-permute-start.2 = (bf16[1,32,1024]{2,1,0:T(8,128)(2,1)S(1)}, bf16[1,32,1024]{2,1,0:T(8,128)(2,1)}, u32[]{:S(2)}, u32[]{:S(2)}) collective-permute-start(bf16[1,32,1024]{2,1,0:T(8,128)(2,1)S(1)} %get-tuple-element.270), channel_id=1, source_target_pairs={{0,3},{1,2},{2,1},{3,0},{4,7},{5,6},{6,5},{7,4},{8,11},{9,10},{10,... | collective-permute-start | bytes 196616 | tf_op jit(solution)/shard_map/while/body/eval_jaxpr/ppermute | solution.py:21
  140.9 14.6 %collective-permute-start.3 = (bf16[1,32,1024]{2,1,0:T(8,128)(2,1)S(1)}, bf16[1,32,1024]{2,1,0:T(8,128)(2,1)}, u32[]{:S(2)}, u32[]{:S(2)}) collective-permute-start(bf16[1,32,1024]{2,1,0:T(8,128)(2,1)S(1)} %get-tuple-element.271), channel_id=1, source_target_pairs={{0,4},{1,5},{2,6},{3,7},{4,0},{5,1},{6,2},{7,3},{8,12},{9,13},{10,... | collective-permute-start | bytes 196616 | tf_op jit(solution)/shard_map/while/body/eval_jaxpr/ppermute | solution.py:21
  142.7 19.7 %collective-permute-start.4 = (bf16[1,32,1024]{2,1,0:T(8,128)(2,1)S(1)}, bf16[1,32,1024]{2,1,0:T(8,128)(2,1)}, u32[]{:S(2)}, u32[]{:S(2)}) collective-permute-start(bf16[1,32,1024]{2,1,0:T(8,128)(2,1)S(1)} %get-tuple-element.272), channel_id=1, source_target_pairs={{0,5},{1,4},{2,7},{3,6},{4,1},{5,0},{6,3},{7,2},{8,13},{9,12},{10,... | collective-permute-start | bytes 196616 | tf_op jit(solution)/shard_map/while/body/eval_jaxpr/ppermute | solution.py:21
  144.2 20.7 %collective-permute-start.5 = (bf16[1,32,1024]{2,1,0:T(8,128)(2,1)S(1)}, bf16[1,32,1024]{2,1,0:T(8,128)(2,1)S(1)}, u32[]{:S(2)}, u32[]{:S(2)}) collective-permute-start(bf16[1,32,1024]{2,1,0:T(8,128)(2,1)S(1)} %get-tuple-element.273), channel_id=1, source_target_pairs={{0,6},{1,7},{2,4},{3,5},{4,2},{5,3},{6,0},{7,1},{8,14},{9,15},{10,... | collective-permute-start | bytes 196616 | tf_op jit(solution)/shard_map/while/body/eval_jaxpr/ppermute | solution.py:21
  147.4 19.8 %collective-permute-start.6 = (bf16[1,32,1024]{2,1,0:T(8,128)(2,1)S(1)}, bf16[1,32,1024]{2,1,0:T(8,128)(2,1)S(1)}, u32[]{:S(2)}, u32[]{:S(2)}) collective-permute-start(bf16[1,32,1024]{2,1,0:T(8,128)(2,1)S(1)} %get-tuple-element.274), channel_id=1, source_target_pairs={{0,7},{1,6},{2,5},{3,4},{4,3},{5,2},{6,1},{7,0},{8,15},{9,14},{10,... | collective-permute-start | bytes 196616 | tf_op jit(solution)/shard_map/while/body/eval_jaxpr/ppermute | solution.py:21
  148.5 18.9 %collective-permute-start.7 = (bf16[1,32,1024]{2,1,0:T(8,128)(2,1)S(1)}, bf16[1,32,1024]{2,1,0:T(8,128)(2,1)S(1)}, u32[]{:S(2)}, u32[]{:S(2)}) collective-permute-start(bf16[1,32,1024]{2,1,0:T(8,128)(2,1)S(1)} %get-tuple-element.275), channel_id=1, source_target_pairs={{0,8},{1,9},{2,10},{3,11},{4,12},{5,13},{6,14},{7,15},{8,0},{9,1},... | collective-permute-start | bytes 196616 | tf_op jit(solution)/shard_map/while/body/eval_jaxpr/ppermute | solution.py:21
  155.5 16.7 %collective-permute-start.8 = (bf16[1,32,1024]{2,1,0:T(8,128)(2,1)S(1)}, bf16[1,32,1024]{2,1,0:T(8,128)(2,1)S(1)}, u32[]{:S(2)}, u32[]{:S(2)}) collective-permute-start(bf16[1,32,1024]{2,1,0:T(8,128)(2,1)S(1)} %get-tuple-element.276), channel_id=1, source_target_pairs={{0,9},{1,8},{2,11},{3,10},{4,13},{5,12},{6,15},{7,14},{8,1},{9,0},... | collective-permute-start | bytes 196616 | tf_op jit(solution)/shard_map/while/body/eval_jaxpr/ppermute | solution.py:21
  162.5 12.3 %collective-permute-start.9 = (bf16[1,32,1024]{2,1,0:T(8,128)(2,1)S(1)}, bf16[1,32,1024]{2,1,0:T(8,128)(2,1)S(1)}, u32[]{:S(2)}, u32[]{:S(2)}) collective-permute-start(bf16[1,32,1024]{2,1,0:T(8,128)(2,1)S(1)} %get-tuple-element.277), channel_id=1, source_target_pairs={{0,10},{1,11},{2,8},{3,9},{4,14},{5,15},{6,12},{7,13},{8,2},{9,3},... | collective-permute-start | bytes 196616 | tf_op jit(solution)/shard_map/while/body/eval_jaxpr/ppermute | solution.py:21
  164.9 13.6 %collective-permute-start.10 = (bf16[1,32,1024]{2,1,0:T(8,128)(2,1)S(1)}, bf16[1,32,1024]{2,1,0:T(8,128)(2,1)S(1)}, u32[]{:S(2)}, u32[]{:S(2)}) collective-permute-start(bf16[1,32,1024]{2,1,0:T(8,128)(2,1)S(1)} %get-tuple-element.278), channel_id=1, source_target_pairs={{0,11},{1,10},{2,9},{3,8},{4,15},{5,14},{6,13},{7,12},{8,3},{9,2},... | collective-permute-start | bytes 196616 | tf_op jit(solution)/shard_map/while/body/eval_jaxpr/ppermute | solution.py:21
  167.3 11.2 %collective-permute-start.11 = (bf16[1,32,1024]{2,1,0:T(8,128)(2,1)S(1)}, bf16[1,32,1024]{2,1,0:T(8,128)(2,1)S(1)}, u32[]{:S(2)}, u32[]{:S(2)}) collective-permute-start(bf16[1,32,1024]{2,1,0:T(8,128)(2,1)S(1)} %get-tuple-element.279), channel_id=1, source_target_pairs={{0,12},{1,13},{2,14},{3,15},{4,8},{5,9},{6,10},{7,11},{8,4},{9,5},... | collective-permute-start | bytes 196616 | tf_op jit(solution)/shard_map/while/body/eval_jaxpr/ppermute | solution.py:21
  167.4 11.2 %collective-permute-start.12 = (bf16[1,32,1024]{2,1,0:T(8,128)(2,1)S(1)}, bf16[1,32,1024]{2,1,0:T(8,128)(2,1)S(1)}, u32[]{:S(2)}, u32[]{:S(2)}) collective-permute-start(bf16[1,32,1024]{2,1,0:T(8,128)(2,1)S(1)} %get-tuple-element.280), channel_id=1, source_target_pairs={{0,13},{1,12},{2,15},{3,14},{4,9},{5,8},{6,11},{7,10},{8,5},{9,4},... | collective-permute-start | bytes 196616 | tf_op jit(solution)/shard_map/while/body/eval_jaxpr/ppermute | solution.py:21
  172.2 7.1 %collective-permute-start.13 = (bf16[1,32,1024]{2,1,0:T(8,128)(2,1)S(1)}, bf16[1,32,1024]{2,1,0:T(8,128)(2,1)S(1)}, u32[]{:S(2)}, u32[]{:S(2)}) collective-permute-start(bf16[1,32,1024]{2,1,0:T(8,128)(2,1)S(1)} %get-tuple-element.281), channel_id=1, source_target_pairs={{0,14},{1,15},{2,12},{3,13},{4,10},{5,11},{6,8},{7,9},{8,6},{9,7},... | collective-permute-start | bytes 196616 | tf_op jit(solution)/shard_map/while/body/eval_jaxpr/ppermute | solution.py:21
  174.8 8.0 %collective-permute-start.14 = (bf16[1,32,1024]{2,1,0:T(8,128)(2,1)S(1)}, bf16[1,32,1024]{2,1,0:T(8,128)(2,1)S(1)}, u32[]{:S(2)}, u32[]{:S(2)}) collective-permute-start(bf16[1,32,1024]{2,1,0:T(8,128)(2,1)S(1)} %get-tuple-element.282), channel_id=1, source_target_pairs={{0,15},{1,14},{2,13},{3,12},{4,11},{5,10},{6,9},{7,8},{8,7},{9,6},... | collective-permute-start | bytes 196616 | tf_op jit(solution)/shard_map/while/body/eval_jaxpr/ppermute | solution.py:21
  187.5 50.7 %all-to-all-start = ((bf16[16,32,1024]{2,1,0:T(8,128)(2,1)}), bf16[16,32,1024]{2,1,0:T(8,128)(2,1)S(1)}, u32[]{:S(2)}, u32[]{:S(2)}) async-start(bf16[16,32,1024]{2,1,0:T(8,128)(2,1)} %bitcast.34), calls=%async_computation | async-start | bytes 2097152 | tf_op jit(solution)/shard_map/while/body/eval_jaxpr/all_to_all | solution.py:39
  192.8 7.1 %collective-permute-start = (bf16[1,32,1024]{2,1,0:T(8,128)(2,1)}, bf16[1,32,1024]{2,1,0:T(8,128)(2,1)}, u32[]{:S(2)}, u32[]{:S(2)}) collective-permute-start(bf16[1,32,1024]{2,1,0:T(8,128)(2,1)} %get-tuple-element.268), channel_id=1, source_target_pairs={{0,1},{1,0},{2,3},{3,2},{4,5},{5,4},{6,7},{7,6},{8,9},{9,8},{10,11... | collective-permute-start | bytes 196616 | tf_op jit(solution)/shard_map/while/body/eval_jaxpr/ppermute | solution.py:21
  194.9 7.8 %collective-permute-start.1 = (bf16[1,32,1024]{2,1,0:T(8,128)(2,1)S(1)}, bf16[1,32,1024]{2,1,0:T(8,128)(2,1)}, u32[]{:S(2)}, u32[]{:S(2)}) collective-permute-start(bf16[1,32,1024]{2,1,0:T(8,128)(2,1)S(1)} %get-tuple-element.269), channel_id=1, source_target_pairs={{0,2},{1,3},{2,0},{3,1},{4,6},{5,7},{6,4},{7,5},{8,10},{9,11},{10,... | collective-permute-start | bytes 196616 | tf_op jit(solution)/shard_map/while/body/eval_jaxpr/ppermute | solution.py:21
  196.1 8.3 %collective-permute-start.2 = (bf16[1,32,1024]{2,1,0:T(8,128)(2,1)S(1)}, bf16[1,32,1024]{2,1,0:T(8,128)(2,1)}, u32[]{:S(2)}, u32[]{:S(2)}) collective-permute-start(bf16[1,32,1024]{2,1,0:T(8,128)(2,1)S(1)} %get-tuple-element.270), channel_id=1, source_target_pairs={{0,3},{1,2},{2,1},{3,0},{4,7},{5,6},{6,5},{7,4},{8,11},{9,10},{10,... | collective-permute-start | bytes 196616 | tf_op jit(solution)/shard_map/while/body/eval_jaxpr/ppermute | solution.py:21
  196.4 14.3 %collective-permute-start.3 = (bf16[1,32,1024]{2,1,0:T(8,128)(2,1)S(1)}, bf16[1,32,1024]{2,1,0:T(8,128)(2,1)}, u32[]{:S(2)}, u32[]{:S(2)}) collective-permute-start(bf16[1,32,1024]{2,1,0:T(8,128)(2,1)S(1)} %get-tuple-element.271), channel_id=1, source_target_pairs={{0,4},{1,5},{2,6},{3,7},{4,0},{5,1},{6,2},{7,3},{8,12},{9,13},{10,... | collective-permute-start | bytes 196616 | tf_op jit(solution)/shard_map/while/body/eval_jaxpr/ppermute | solution.py:21
  198.1 19.7 %collective-permute-start.4 = (bf16[1,32,1024]{2,1,0:T(8,128)(2,1)S(1)}, bf16[1,32,1024]{2,1,0:T(8,128)(2,1)}, u32[]{:S(2)}, u32[]{:S(2)}) collective-permute-start(bf16[1,32,1024]{2,1,0:T(8,128)(2,1)S(1)} %get-tuple-element.272), channel_id=1, source_target_pairs={{0,5},{1,4},{2,7},{3,6},{4,1},{5,0},{6,3},{7,2},{8,13},{9,12},{10,... | collective-permute-start | bytes 196616 | tf_op jit(solution)/shard_map/while/body/eval_jaxpr/ppermute | solution.py:21
  199.9 20.3 %collective-permute-start.5 = (bf16[1,32,1024]{2,1,0:T(8,128)(2,1)S(1)}, bf16[1,32,1024]{2,1,0:T(8,128)(2,1)S(1)}, u32[]{:S(2)}, u32[]{:S(2)}) collective-permute-start(bf16[1,32,1024]{2,1,0:T(8,128)(2,1)S(1)} %get-tuple-element.273), channel_id=1, source_target_pairs={{0,6},{1,7},{2,4},{3,5},{4,2},{5,3},{6,0},{7,1},{8,14},{9,15},{10,... | collective-permute-start | bytes 196616 | tf_op jit(solution)/shard_map/while/body/eval_jaxpr/ppermute | solution.py:21
  202.8 19.8 %collective-permute-start.6 = (bf16[1,32,1024]{2,1,0:T(8,128)(2,1)S(1)}, bf16[1,32,1024]{2,1,0:T(8,128)(2,1)S(1)}, u32[]{:S(2)}, u32[]{:S(2)}) collective-permute-start(bf16[1,32,1024]{2,1,0:T(8,128)(2,1)S(1)} %get-tuple-element.274), channel_id=1, source_target_pairs={{0,7},{1,6},{2,5},{3,4},{4,3},{5,2},{6,1},{7,0},{8,15},{9,14},{10,... | collective-permute-start | bytes 196616 | tf_op jit(solution)/shard_map/while/body/eval_jaxpr/ppermute | solution.py:21
  204.3 18.4 %collective-permute-start.7 = (bf16[1,32,1024]{2,1,0:T(8,128)(2,1)S(1)}, bf16[1,32,1024]{2,1,0:T(8,128)(2,1)S(1)}, u32[]{:S(2)}, u32[]{:S(2)}) collective-permute-start(bf16[1,32,1024]{2,1,0:T(8,128)(2,1)S(1)} %get-tuple-element.275), channel_id=1, source_target_pairs={{0,8},{1,9},{2,10},{3,11},{4,12},{5,13},{6,14},{7,15},{8,0},{9,1},... | collective-permute-start | bytes 196616 | tf_op jit(solution)/shard_map/while/body/eval_jaxpr/ppermute | solution.py:21
  210.7 16.8 %collective-permute-start.8 = (bf16[1,32,1024]{2,1,0:T(8,128)(2,1)S(1)}, bf16[1,32,1024]{2,1,0:T(8,128)(2,1)S(1)}, u32[]{:S(2)}, u32[]{:S(2)}) collective-permute-start(bf16[1,32,1024]{2,1,0:T(8,128)(2,1)S(1)} %get-tuple-element.276), channel_id=1, source_target_pairs={{0,9},{1,8},{2,11},{3,10},{4,13},{5,12},{6,15},{7,14},{8,1},{9,0},... | collective-permute-start | bytes 196616 | tf_op jit(solution)/shard_map/while/body/eval_jaxpr/ppermute | solution.py:21
  217.8 12.4 %collective-permute-start.9 = (bf16[1,32,1024]{2,1,0:T(8,128)(2,1)S(1)}, bf16[1,32,1024]{2,1,0:T(8,128)(2,1)S(1)}, u32[]{:S(2)}, u32[]{:S(2)}) collective-permute-start(bf16[1,32,1024]{2,1,0:T(8,128)(2,1)S(1)} %get-tuple-element.277), channel_id=1, source_target_pairs={{0,10},{1,11},{2,8},{3,9},{4,14},{5,15},{6,12},{7,13},{8,2},{9,3},... | collective-permute-start | bytes 196616 | tf_op jit(solution)/shard_map/while/body/eval_jaxpr/ppermute | solution.py:21
  220.2 13.6 %collective-permute-start.10 = (bf16[1,32,1024]{2,1,0:T(8,128)(2,1)S(1)}, bf16[1,32,1024]{2,1,0:T(8,128)(2,1)S(1)}, u32[]{:S(2)}, u32[]{:S(2)}) collective-permute-start(bf16[1,32,1024]{2,1,0:T(8,128)(2,1)S(1)} %get-tuple-element.278), channel_id=1, source_target_pairs={{0,11},{1,10},{2,9},{3,8},{4,15},{5,14},{6,13},{7,12},{8,3},{9,2},... | collective-permute-start | bytes 196616 | tf_op jit(solution)/shard_map/while/body/eval_jaxpr/ppermute | solution.py:21
  222.6 11.2 %collective-permute-start.11 = (bf16[1,32,1024]{2,1,0:T(8,128)(2,1)S(1)}, bf16[1,32,1024]{2,1,0:T(8,128)(2,1)S(1)}, u32[]{:S(2)}, u32[]{:S(2)}) collective-permute-start(bf16[1,32,1024]{2,1,0:T(8,128)(2,1)S(1)} %get-tuple-element.279), channel_id=1, source_target_pairs={{0,12},{1,13},{2,14},{3,15},{4,8},{5,9},{6,10},{7,11},{8,4},{9,5},... | collective-permute-start | bytes 196616 | tf_op jit(solution)/shard_map/while/body/eval_jaxpr/ppermute | solution.py:21
  222.7 11.2 %collective-permute-start.12 = (bf16[1,32,1024]{2,1,0:T(8,128)(2,1)S(1)}, bf16[1,32,1024]{2,1,0:T(8,128)(2,1)S(1)}, u32[]{:S(2)}, u32[]{:S(2)}) collective-permute-start(bf16[1,32,1024]{2,1,0:T(8,128)(2,1)S(1)} %get-tuple-element.280), channel_id=1, source_target_pairs={{0,13},{1,12},{2,15},{3,14},{4,9},{5,8},{6,11},{7,10},{8,5},{9,4},... | collective-permute-start | bytes 196616 | tf_op jit(solution)/shard_map/while/body/eval_jaxpr/ppermute | solution.py:21
  227.5 7.1 %collective-permute-start.13 = (bf16[1,32,1024]{2,1,0:T(8,128)(2,1)S(1)}, bf16[1,32,1024]{2,1,0:T(8,128)(2,1)S(1)}, u32[]{:S(2)}, u32[]{:S(2)}) collective-permute-start(bf16[1,32,1024]{2,1,0:T(8,128)(2,1)S(1)} %get-tuple-element.281), channel_id=1, source_target_pairs={{0,14},{1,15},{2,12},{3,13},{4,10},{5,11},{6,8},{7,9},{8,6},{9,7},... | collective-permute-start | bytes 196616 | tf_op jit(solution)/shard_map/while/body/eval_jaxpr/ppermute | solution.py:21
  230.2 8.0 %collective-permute-start.14 = (bf16[1,32,1024]{2,1,0:T(8,128)(2,1)S(1)}, bf16[1,32,1024]{2,1,0:T(8,128)(2,1)S(1)}, u32[]{:S(2)}, u32[]{:S(2)}) collective-permute-start(bf16[1,32,1024]{2,1,0:T(8,128)(2,1)S(1)} %get-tuple-element.282), channel_id=1, source_target_pairs={{0,15},{1,14},{2,13},{3,12},{4,11},{5,10},{6,9},{7,8},{8,7},{9,6},... | collective-permute-start | bytes 196616 | tf_op jit(solution)/shard_map/while/body/eval_jaxpr/ppermute | solution.py:21
  (3 other events, 14.6 us)
Sparse Core Ops, SparseCore 0:
  130.0 10.4 reduce-scatter.4
  243.8 10.5 reduce-scatter.2
